TPU v7x, 128 devices: a whole 4x4x4 slice. The times are simulated.
128 devices in a mesh: row: 16 (over z, y_hi, core), col: 8 (over x, y_lo).
Axes of the slice: x: 4, y: 4 (y_hi: 2, y_lo: 2; y = y_hi * 2 + y_lo), z: 4, core: 2. Of those that a mesh axis runs over, the one named last changes fastest.
Arguments:
- observed: int32 [4096, 32, 2048], P('row', None, 'col'), may hold values 0 or 1
- first_factor: float32 [4096, 256], P(('row', 'col')), may hold values from -1.35 to 1.35
- second_factor: float32 [2048, 256], P(('col', 'row')), may hold values from -1.35 to 1.35
- third_factor: float32 [32, 256], replicated, may hold values from -1.35 to 1.35
Outputs:
- first_out: float32 [4096, 256], P(('row', 'col'))
- second_out: float32 [2048, 256], P(('col', 'row'))
- third_out: float32 [32, 256], replicated
All inputs are finite; a program needn't handle non-finite values. No bound on the sum of `observed` on one device may be relied on, other than what follows from the above.
Results may differ from a plain program's by a relative error of at most 0.0003.
Values sent between devices are 32-bit elements; how exact they have to be, the bound alone decides.
A program may use at most 128 MiB of HBM per device.

v0:
```python
import functools

import jax
import jax.numpy as jnp
from jax import lax
from jax.experimental import pallas as pl
from jax.experimental.pallas import tpu as pltpu
from jax.sharding import PartitionSpec as P

STEPS = 2
step_rate = 48.0
f32, bf16 = jnp.float32, jnp.bfloat16
MESH = pl.DeviceIdType.MESH
NT = (((1,), (1,)), ((), ()))
NN = (((1,), (0,)), ((), ()))
TN = (((0,), (0,)), ((), ()))
LANES = 128
SUBLANES = 8
CHUNK = 16


def dot(a, b, dims):
    return lax.dot_general(a, b, dims, preferred_element_type=f32)


def split(x):
    high = x.astype(bf16)
    return high, (x - high.astype(f32)).astype(bf16)


def kernel(
    n_row, n_col, rates,
    obs_hbm, a_in, b_in, c_in,
    a_out, b_out, c_out,
    obs, a_all, b_all, c_now, b_high, b_low,
    ga, ga_got, gb, gb_got, gc, gc_part, gc_got, gc_sum, c_new,
    pair0, pair1, der0, der1,
    obs_sem, a_send, a_recv, b_send, b_recv, ga_send, ga_recv, gb_send, gb_recv,
    c1_send, c1_recv, c2_send, c2_recv, c3_send, c3_recv,
):
    row, col = lax.axis_index("row"), lax.axis_index("col")
    rate_one, rate_two, rate_three = rates
    depth, rank = c_in.shape
    tiles = [(k, l) for k in range(depth // SUBLANES) for l in range(rank // LANES)]

    def to_col(src, dst, send, recv, peer):
        return pltpu.make_async_remote_copy(
            src_ref=src, dst_ref=dst, send_sem=send, recv_sem=recv,
            device_id={"col": peer}, device_id_type=MESH,
        )

    def to_row(src, dst, send, recv, peer):
        return pltpu.make_async_remote_copy(
            src_ref=src, dst_ref=dst, send_sem=send, recv_sem=recv,
            device_id={"row": peer}, device_id_type=MESH,
        )

    def col_peer(d):
        return lax.rem(col + d, n_col)

    def row_peer(d):
        return lax.rem(row + d, n_row)

    rows_here = a_in.shape[0]

    def obs_copy(block):
        part = pl.ds(pl.multiple_of(block * rows_here, rows_here), rows_here)
        return pltpu.make_async_copy(obs_hbm.at[part], obs.at[part], obs_sem.at[block])

    barrier = pltpu.get_barrier_semaphore()
    for d in range(1, n_row):
        pl.semaphore_signal(barrier, inc=1, device_id={"row": row_peer(d)}, device_id_type=MESH)
    for d in range(1, n_col):
        pl.semaphore_signal(barrier, inc=1, device_id={"col": col_peer(d)}, device_id_type=MESH)
    for d in range(n_col):
        obs_copy(col_peer(d)).start()
    pl.semaphore_wait(barrier, n_row + n_col - 2)

    def send_b(step, src):
        for d in range(1, n_row):
            to_row(src, b_all.at[step, row], b_send.at[step, d], b_recv.at[step, row], row_peer(d)).start()

    def send_a(step, src):
        for d in range(1, n_col):
            to_col(src, a_all.at[step, col], a_send.at[step, d], a_recv.at[step, col], col_peer(d)).start()

    def wait_a(step, block):
        here = a_all.at[step, block]
        to_col(here, here, a_send.at[step, 0], a_recv.at[step, block], col_peer(1)).wait_recv()

    send_b(0, b_in)
    send_a(0, a_in)
    a_all[0, col] = a_in[...]
    b_all[0, row] = b_in[...]
    c_now[...] = c_in[...]

    for step in range(STEPS):
        for d in range(1, n_row):
            here = b_all.at[step, row_peer(d)]
            to_row(here, here, b_send.at[step, 0], b_recv.at[step, row_peer(d)], row_peer(1)).wait_recv()
        high, low = split(0.5 * b_all[step].reshape(n_row * b_in.shape[0], rank))
        b_high[...], b_low[...] = high, low
        gb[step] = jnp.zeros(gb.shape[1:], f32)
        gc[...] = jnp.zeros(gc.shape, f32)

        def rows_of(block, half):
            return a_all[step, block, pl.ds(half * CHUNK, CHUNK), :]

        def front(block, half, pair, der):
            start = pl.multiple_of(block * rows_here + half * CHUNK, CHUNK)
            seen = obs[pl.ds(start, CHUNK)].reshape(CHUNK * depth, -1)
            paired = (rows_of(block, half)[:, None, :] * c_now[...][None]).reshape(CHUNK * depth, rank)
            p_high, p_low = split(paired)
            half_logits = (
                dot(p_high, b_high[...], NT) + dot(p_low, b_high[...], NT) + dot(p_high, b_low[...], NT)
            )
            d_high, d_low = split(jnp.tanh(half_logits) + (1.0 - 2.0 * seen.astype(f32)))
            pair[0], pair[1] = p_high, p_low
            der[0], der[1] = d_high, d_low

        def back(block, half, pair, der):
            p_high, p_low, d_high, d_low = pair[0], pair[1], der[0], der[1]
            part_b = dot(d_high, p_high, TN) + dot(d_high, p_low, TN) + dot(d_low, p_high, TN)
            carried = dot(d_high, b_high[...], NN) + dot(d_high, b_low[...], NN) + dot(d_low, b_high[...], NN)
            carried = carried.reshape(CHUNK, depth, rank)
            ga[step, block, pl.ds(half * CHUNK, CHUNK), :] = jnp.sum(carried * c_now[...][None], axis=1)
            gc[...] += jnp.sum(carried * rows_of(block, half)[:, None, :], axis=0)
            gb[step] += part_b.reshape(gb.shape[1:])

        def send_ga(d):
            owner = col_peer(d)
            to_col(
                ga.at[step, owner], ga_got.at[step, col], ga_send.at[step, d], ga_recv.at[step, col], owner
            ).start()

        if step == 0:
            obs_copy(col).wait()
        front(col, 0, pair0, der0)

        def block_body(d, carry):
            block, later = col_peer(d), col_peer(d + 1)
            wait_a(step, later)
            if step == 0:
                obs_copy(later).wait()
            front(block, 1, pair1, der1)
            back(block, 0, pair0, der0)
            front(later, 0, pair0, der0)
            back(block, 1, pair1, der1)

            @pl.when(d > 0)
            def _():
                send_ga(d)

            return carry

        lax.fori_loop(0, n_col - 1, block_body, 0)
        last = col_peer(n_col - 1)
        front(last, 1, pair1, der1)
        back(last, 0, pair0, der0)
        back(last, 1, pair1, der1)

        for t, (k, l) in enumerate(tiles):
            gc_part[step, t] = gc[k * SUBLANES : (k + 1) * SUBLANES, l * LANES : (l + 1) * LANES]
        for d in range(1, n_col):
            owner = col_peer(d)
            to_col(
                gc_part.at[step, owner], gc_got.at[step, col], c1_send.at[step, d], c1_recv.at[step, col], owner
            ).start()
        for d in range(1, n_row):
            owner = row_peer(d)
            to_row(
                gb.at[step, owner], gb_got.at[step, row], gb_send.at[step, d], gb_recv.at[step, row], owner
            ).start()
        send_ga(n_col - 1)

        total = gc_part[step, col]
        for d in range(1, n_col):
            here = gc_got.at[step, col_peer(d)]
            to_col(here, here, c1_send.at[step, 0], c1_recv.at[step, col_peer(d)], col_peer(1)).wait_recv()
            total = total + here[...]
        gc_sum[step, row] = total
        for d in range(1, n_row):
            here = gc_sum.at[step, row]
            to_row(here, here, c2_send.at[step, d], c2_recv.at[step, row], row_peer(d)).start()

        total = gb[step, row]
        for d in range(1, n_row):
            here = gb_got.at[step, row_peer(d)]
            to_row(here, here, gb_send.at[step, 0], gb_recv.at[step, row_peer(d)], row_peer(1)).wait_recv()
            total = total + here[...]
        updated = b_all[step, row] - rate_two * total
        if step + 1 < STEPS:
            b_all[step + 1, row] = updated
            send_b(step + 1, b_all.at[step + 1, row])
        else:
            b_out[...] = updated

        total = ga[step, col]
        for d in range(1, n_col):
            here = ga_got.at[step, col_peer(d)]
            to_col(here, here, ga_send.at[step, 0], ga_recv.at[step, col_peer(d)], col_peer(1)).wait_recv()
            total = total + here[...]
        updated = a_all[step, col] - rate_one * total
        if step + 1 < STEPS:
            a_all[step + 1, col] = updated
            send_a(step + 1, a_all.at[step + 1, col])
        else:
            a_out[...] = updated

        total = gc_sum[step, row]
        for d in range(1, n_row):
            here = gc_sum.at[step, row_peer(d)]
            to_row(here, here, c2_send.at[step, 0], c2_recv.at[step, row_peer(d)], row_peer(1)).wait_recv()
            total = total + here[...]
        for t, (k, l) in enumerate(tiles):
            gc_part[step + 1, t] = c_now[k * SUBLANES : (k + 1) * SUBLANES, l * LANES : (l + 1) * LANES]
        c_new[step, col] = gc_part[step + 1, col] - rate_three * total
        for d in range(1, n_col):
            here = c_new.at[step, col]
            to_col(here, here, c3_send.at[step, d], c3_recv.at[step, col], col_peer(d)).start()
        for d in range(1, n_col):
            here = c_new.at[step, col_peer(d)]
            to_col(here, here, c3_send.at[step, 0], c3_recv.at[step, col_peer(d)], col_peer(1)).wait_recv()
        target = c_out if step + 1 == STEPS else c_now
        for t, (k, l) in enumerate(tiles):
            target[k * SUBLANES : (k + 1) * SUBLANES, l * LANES : (l + 1) * LANES] = c_new[step, t]

    for step in range(STEPS):
        for d in range(1, n_col):
            to_col(ga.at[step, 0], ga.at[step, 0], ga_send.at[step, d], ga_recv.at[step, 0], col_peer(d)).wait_send()
            for part, sem in ((gc_part, c1_send), (c_new, c3_send)):
                here = part.at[step, 0]
                to_col(here, here, sem.at[step, d], c1_recv.at[step, 0], col_peer(d)).wait_send()
            here = a_all.at[step, 0]
            to_col(here, here, a_send.at[step, d], a_recv.at[step, 0], col_peer(d)).wait_send()
        for d in range(1, n_row):
            for part, sem in ((gb, gb_send), (gc_sum, c2_send), (b_all, b_send)):
                here = part.at[step, 0]
                to_row(here, here, sem.at[step, d], gb_recv.at[step, 0], row_peer(d)).wait_send()


def per_device(observed, first_factor, second_factor, third_factor):
    n_row, n_col = lax.axis_size("row"), lax.axis_size("col")
    first_here, depth, second_here = observed.shape
    rank = third_factor.shape[1]
    rates = (
        step_rate / (second_here * n_col * depth),
        0.5 * step_rate / (first_here * n_row * depth),
        step_rate / (first_here * n_row * second_here * n_col),
    )
    a_rows, b_rows = first_factor.shape[0], second_factor.shape[0]
    tile = (SUBLANES, LANES)
    dma = pltpu.SemaphoreType.DMA
    vmem = pl.BlockSpec(memory_space=pltpu.VMEM)
    return pl.pallas_call(
        functools.partial(kernel, n_row, n_col, rates),
        name="cp_steps",
        out_shape=[
            jax.ShapeDtypeStruct(first_factor.shape, f32),
            jax.ShapeDtypeStruct(second_factor.shape, f32),
            jax.ShapeDtypeStruct(third_factor.shape, f32),
        ],
        in_specs=[pl.BlockSpec(memory_space=pl.ANY), vmem, vmem, vmem],
        out_specs=[vmem] * 3,
        scratch_shapes=[
            pltpu.VMEM(observed.shape, jnp.int32),
            pltpu.VMEM((STEPS, n_col, a_rows, rank), f32),
            pltpu.VMEM((STEPS, n_row, b_rows, rank), f32),
            pltpu.VMEM((depth, rank), f32),
            pltpu.VMEM((second_here, rank), bf16),
            pltpu.VMEM((second_here, rank), bf16),
            pltpu.VMEM((STEPS, n_col, a_rows, rank), f32),
            pltpu.VMEM((STEPS, n_col, a_rows, rank), f32),
            pltpu.VMEM((STEPS, n_row, b_rows, rank), f32),
            pltpu.VMEM((STEPS, n_row, b_rows, rank), f32),
            pltpu.VMEM((depth, rank), f32),
            pltpu.VMEM((STEPS + 1, n_col, *tile), f32),
            pltpu.VMEM((STEPS, n_col, *tile), f32),
            pltpu.VMEM((STEPS, n_row, *tile), f32),
            pltpu.VMEM((STEPS, n_col, *tile), f32),
            pltpu.VMEM((2, CHUNK * depth, rank), bf16),
            pltpu.VMEM((2, CHUNK * depth, rank), bf16),
            pltpu.VMEM((2, CHUNK * depth, second_here), bf16),
            pltpu.VMEM((2, CHUNK * depth, second_here), bf16),
            dma((n_col,)),
        ]
        + [dma((STEPS, n)) for n in (n_col, n_row, n_col, n_row, n_col, n_row, n_col) for _ in range(2)],
        compiler_params=pltpu.CompilerParams(
            collective_id=0, has_side_effects=True, vmem_limit_bytes=62 * 2**20
        ),
    )(observed, first_factor, second_factor, third_factor)


def solution(mesh):
    return jax.shard_map(
        per_device,
        mesh=mesh,
        in_specs=(P("row", None, "col"), P(("row", "col"), None), P(("col", "row"), None), P()),
        out_specs=(P(("row", "col"), None), P(("col", "row"), None), P()),
        check_vma=False,
    )
```

profile of v0, /device:TPU:1, one launch (start us, length us, event | category | flops | bytes accessed | tf_op | source)
XLA Modules:
  0.0 78.3 jit_solution(9402350457537036409)
XLA Ops:
  0.6 73.6 %cp_steps.1 = (f32[32,256]{1,0:T(8,128)}, f32[16,256]{1,0:T(8,128)}, f32[32,256]{1,0:T(8,128)}) custom-call(s32[256,32,256]{2,1,0:T(8,128)} %obs_hbm.1, f32[32,256]{1,0:T(8,128)} %a_in.1, f32[16,256]{1,0:T(8,128)} %b_in.1, f32[32,256]{1,0:T(8,128)} %c_in.1), custom_call_target="tpu_custom_call" | custom-call | tf_op jit(solution)/shard_map/cp_steps/pallas_call | solution.py:255
  74.3 1.4 %copy.10 = f32[32,256]{1,0:T(8,128)} copy(f32[32,256]{1,0:T(8,128)} %get-tuple-element.6) | data formatting | bytes 65536
  75.6 1.3 %copy.11 = f32[16,256]{1,0:T(8,128)} copy(f32[16,256]{1,0:T(8,128)} %get-tuple-element.7) | data formatting | bytes 32768
  76.9 1.4 %copy.12 = f32[32,256]{1,0:T(8,128)} copy(f32[32,256]{1,0:T(8,128)} %get-tuple-element.8) | data formatting | bytes 65536
where the time goes:
time: 78.7 us; the launch traced here: 78.3 us
  Pallas kernels  73.6 us (94%)
  local copies, waits for them, and re-layouts  4.07 us (5%)
    pallas_call x1, Pallas kernels, per_device(): pl.pallas_call(functools.partial(kernel, n_row, n_col, rates), name='cp_s...  73.6 us
    unnamed x3, local copies, waits for them, and re-layouts  4.07 us

commit v1 on v0

--- a/solution.py
+++ b/solution.py
@@ -11,11 +11,11 @@
 step_rate = 48.0
 f32, bf16 = jnp.float32, jnp.bfloat16
 MESH = pl.DeviceIdType.MESH
-NT = (((1,), (1,)), ((), ()))
 NN = (((1,), (0,)), ((), ()))
 TN = (((0,), (0,)), ((), ()))
 LANES = 128
 SUBLANES = 8
+MIDDLE = ("b", "a", "c")
 CHUNK = 16
 
 
@@ -32,8 +32,8 @@
     n_row, n_col, rates,
     obs_hbm, a_in, b_in, c_in,
     a_out, b_out, c_out,
-    obs, a_all, b_all, c_now, b_high, b_low,
-    ga, ga_got, gb, gb_got, gc, gc_part, gc_got, gc_sum, c_new,
+    obs, a_all, b_all, c_now, b_high, b_low, bt_high, bt_low,
+    ga, ga_got, gb, gb_got, gc, gc_part, gc_got, gc_sum, c_new, c_tile,
     pair0, pair1, der0, der1,
     obs_sem, a_send, a_recv, b_send, b_recv, ga_send, ga_recv, gb_send, gb_recv,
     c1_send, c1_recv, c2_send, c2_recv, c3_send, c3_recv,
@@ -81,7 +81,7 @@
             to_row(src, b_all.at[step, row], b_send.at[step, d], b_recv.at[step, row], row_peer(d)).start()
 
     def send_a(step, src):
-        for d in range(1, n_col):
+        for d in reversed(range(1, n_col)):
             to_col(src, a_all.at[step, col], a_send.at[step, d], a_recv.at[step, col], col_peer(d)).start()
 
     def wait_a(step, block):
@@ -94,12 +94,23 @@
     b_all[0, row] = b_in[...]
     c_now[...] = c_in[...]
 
+    def all_left(step):
+        for d in range(1, n_col):
+            for part, sem in ((ga, ga_send), (gc_part, c1_send), (c_new, c3_send)):
+                here = part.at[step, 0]
+                to_col(here, here, sem.at[step, d], a_recv.at[step, 0], col_peer(d)).wait_send()
+        for d in range(1, n_row):
+            for part, sem in ((gb, gb_send), (gc_sum, c2_send)):
+                here = part.at[step, 0]
+                to_row(here, here, sem.at[step, d], gb_recv.at[step, 0], row_peer(d)).wait_send()
+
     for step in range(STEPS):
         for d in range(1, n_row):
             here = b_all.at[step, row_peer(d)]
             to_row(here, here, b_send.at[step, 0], b_recv.at[step, row_peer(d)], row_peer(1)).wait_recv()
-        high, low = split(0.5 * b_all[step].reshape(n_row * b_in.shape[0], rank))
-        b_high[...], b_low[...] = high, low
+        halved = 0.5 * b_all[step].reshape(n_row * b_in.shape[0], rank)
+        b_high[...], b_low[...] = split(halved)
+        bt_high[...], bt_low[...] = split(halved.T)
         gb[step] = jnp.zeros(gb.shape[1:], f32)
         gc[...] = jnp.zeros(gc.shape, f32)
 
@@ -112,7 +123,7 @@
             paired = (rows_of(block, half)[:, None, :] * c_now[...][None]).reshape(CHUNK * depth, rank)
             p_high, p_low = split(paired)
             half_logits = (
-                dot(p_high, b_high[...], NT) + dot(p_low, b_high[...], NT) + dot(p_high, b_low[...], NT)
+                dot(p_high, bt_high[...], NN) + dot(p_low, bt_high[...], NN) + dot(p_high, bt_low[...], NN)
             )
             d_high, d_low = split(jnp.tanh(half_logits) + (1.0 - 2.0 * seen.astype(f32)))
             pair[0], pair[1] = p_high, p_low
@@ -161,82 +172,96 @@
 
         for t, (k, l) in enumerate(tiles):
             gc_part[step, t] = gc[k * SUBLANES : (k + 1) * SUBLANES, l * LANES : (l + 1) * LANES]
+            c_tile[t] = c_now[k * SUBLANES : (k + 1) * SUBLANES, l * LANES : (l + 1) * LANES]
         for d in range(1, n_col):
             owner = col_peer(d)
             to_col(
                 gc_part.at[step, owner], gc_got.at[step, col], c1_send.at[step, d], c1_recv.at[step, col], owner
             ).start()
-        for d in range(1, n_row):
-            owner = row_peer(d)
-            to_row(
-                gb.at[step, owner], gb_got.at[step, row], gb_send.at[step, d], gb_recv.at[step, row], owner
-            ).start()
-        send_ga(n_col - 1)
-
-        total = gc_part[step, col]
+        gc_got[step, col] = gc_part[step, col]
+        final = step + 1 == STEPS
+
+        def send_gb():
+            for d in range(1, n_row):
+                owner = row_peer(d)
+                to_row(
+                    gb.at[step, owner], gb_got.at[step, row], gb_send.at[step, d], gb_recv.at[step, row], owner
+                ).start()
+            send_ga(n_col - 1)
+
+        if not final:
+            send_gb()
         for d in range(1, n_col):
             here = gc_got.at[step, col_peer(d)]
             to_col(here, here, c1_send.at[step, 0], c1_recv.at[step, col_peer(d)], col_peer(1)).wait_recv()
-            total = total + here[...]
-        gc_sum[step, row] = total
+        gc_sum[step, row] = sum(gc_got[step, p] for p in range(n_col))
         for d in range(1, n_row):
             here = gc_sum.at[step, row]
             to_row(here, here, c2_send.at[step, d], c2_recv.at[step, row], row_peer(d)).start()
-
-        total = gb[step, row]
-        for d in range(1, n_row):
-            here = gb_got.at[step, row_peer(d)]
-            to_row(here, here, gb_send.at[step, 0], gb_recv.at[step, row_peer(d)], row_peer(1)).wait_recv()
-            total = total + here[...]
-        updated = b_all[step, row] - rate_two * total
-        if step + 1 < STEPS:
-            b_all[step + 1, row] = updated
-            send_b(step + 1, b_all.at[step + 1, row])
-        else:
-            b_out[...] = updated
-
-        total = ga[step, col]
-        for d in range(1, n_col):
-            here = ga_got.at[step, col_peer(d)]
-            to_col(here, here, ga_send.at[step, 0], ga_recv.at[step, col_peer(d)], col_peer(1)).wait_recv()
-            total = total + here[...]
-        updated = a_all[step, col] - rate_one * total
-        if step + 1 < STEPS:
-            a_all[step + 1, col] = updated
-            send_a(step + 1, a_all.at[step + 1, col])
-        else:
-            a_out[...] = updated
-
-        total = gc_sum[step, row]
-        for d in range(1, n_row):
-            here = gc_sum.at[step, row_peer(d)]
-            to_row(here, here, c2_send.at[step, 0], c2_recv.at[step, row_peer(d)], row_peer(1)).wait_recv()
-            total = total + here[...]
-        for t, (k, l) in enumerate(tiles):
-            gc_part[step + 1, t] = c_now[k * SUBLANES : (k + 1) * SUBLANES, l * LANES : (l + 1) * LANES]
-        c_new[step, col] = gc_part[step + 1, col] - rate_three * total
-        for d in range(1, n_col):
-            here = c_new.at[step, col]
-            to_col(here, here, c3_send.at[step, d], c3_recv.at[step, col], col_peer(d)).start()
+        if final:
+            send_gb()
+            for earlier in range(STEPS):
+                for d in range(1, n_col):
+                    here = a_all.at[earlier, 0]
+                    to_col(here, here, a_send.at[earlier, d], a_recv.at[earlier, 0], col_peer(d)).wait_send()
+                for d in range(1, n_row):
+                    here = b_all.at[earlier, 0]
+                    to_row(here, here, b_send.at[earlier, d], b_recv.at[earlier, 0], row_peer(d)).wait_send()
+            for earlier in range(STEPS - 1):
+                all_left(earlier)
+
+        def update_a():
+            total = ga[step, col]
+            for d in range(1, n_col):
+                here = ga_got.at[step, col_peer(d)]
+                to_col(here, here, ga_send.at[step, 0], ga_recv.at[step, col_peer(d)], col_peer(1)).wait_recv()
+                total = total + here[...]
+            updated = a_all[step, col] - rate_one * total
+            if final:
+                a_out[...] = updated
+            else:
+                a_all[step + 1, col] = updated
+                send_a(step + 1, a_all.at[step + 1, col])
+
+        def update_b():
+            total = gb[step, row]
+            for d in range(1, n_row):
+                here = gb_got.at[step, row_peer(d)]
+                to_row(here, here, gb_send.at[step, 0], gb_recv.at[step, row_peer(d)], row_peer(1)).wait_recv()
+                total = total + here[...]
+            updated = b_all[step, row] - rate_two * total
+            if final:
+                b_out[...] = updated
+            else:
+                b_all[step + 1, row] = updated
+                send_b(step + 1, b_all.at[step + 1, row])
+
+        def finish_c():
+            for d in range(1, n_row):
+                here = gc_sum.at[step, row_peer(d)]
+                to_row(here, here, c2_send.at[step, 0], c2_recv.at[step, row_peer(d)], row_peer(1)).wait_recv()
+            total = sum(gc_sum[step, p] for p in range(n_row))
+            c_new[step, col] = c_tile[col] - rate_three * total
+            for d in range(1, n_col):
+                here = c_new.at[step, col]
+                to_col(here, here, c3_send.at[step, d], c3_recv.at[step, col], col_peer(d)).start()
+
+        for stage in MIDDLE if not final else ("c", "b", "a"):
+            {"a": update_a, "b": update_b, "c": finish_c}[stage]()
+        if final:
+            all_left(step)
         for d in range(1, n_col):
             here = c_new.at[step, col_peer(d)]
             to_col(here, here, c3_send.at[step, 0], c3_recv.at[step, col_peer(d)], col_peer(1)).wait_recv()
-        target = c_out if step + 1 == STEPS else c_now
+        target = c_out if final else c_now
         for t, (k, l) in enumerate(tiles):
             target[k * SUBLANES : (k + 1) * SUBLANES, l * LANES : (l + 1) * LANES] = c_new[step, t]
 
-    for step in range(STEPS):
-        for d in range(1, n_col):
-            to_col(ga.at[step, 0], ga.at[step, 0], ga_send.at[step, d], ga_recv.at[step, 0], col_peer(d)).wait_send()
-            for part, sem in ((gc_part, c1_send), (c_new, c3_send)):
-                here = part.at[step, 0]
-                to_col(here, here, sem.at[step, d], c1_recv.at[step, 0], col_peer(d)).wait_send()
-            here = a_all.at[step, 0]
-            to_col(here, here, a_send.at[step, d], a_recv.at[step, 0], col_peer(d)).wait_send()
-        for d in range(1, n_row):
-            for part, sem in ((gb, gb_send), (gc_sum, c2_send), (b_all, b_send)):
-                here = part.at[step, 0]
-                to_row(here, here, sem.at[step, d], gb_recv.at[step, 0], row_peer(d)).wait_send()
+
+def hand_over(*refs):
+    n = len(refs) // 2
+    for source, target in zip(refs[:n], refs[n:]):
+        target[...] = source[...]
 
 
 def per_device(observed, first_factor, second_factor, third_factor):
@@ -252,14 +277,11 @@
     tile = (SUBLANES, LANES)
     dma = pltpu.SemaphoreType.DMA
     vmem = pl.BlockSpec(memory_space=pltpu.VMEM)
-    return pl.pallas_call(
+    results = [jax.ShapeDtypeStruct(x.shape, f32) for x in (first_factor, second_factor, third_factor)]
+    factors = pl.pallas_call(
         functools.partial(kernel, n_row, n_col, rates),
         name="cp_steps",
-        out_shape=[
-            jax.ShapeDtypeStruct(first_factor.shape, f32),
-            jax.ShapeDtypeStruct(second_factor.shape, f32),
-            jax.ShapeDtypeStruct(third_factor.shape, f32),
-        ],
+        out_shape=results,
         in_specs=[pl.BlockSpec(memory_space=pl.ANY), vmem, vmem, vmem],
         out_specs=[vmem] * 3,
         scratch_shapes=[
@@ -269,15 +291,18 @@
             pltpu.VMEM((depth, rank), f32),
             pltpu.VMEM((second_here, rank), bf16),
             pltpu.VMEM((second_here, rank), bf16),
+            pltpu.VMEM((rank, second_here), bf16),
+            pltpu.VMEM((rank, second_here), bf16),
             pltpu.VMEM((STEPS, n_col, a_rows, rank), f32),
             pltpu.VMEM((STEPS, n_col, a_rows, rank), f32),
             pltpu.VMEM((STEPS, n_row, b_rows, rank), f32),
             pltpu.VMEM((STEPS, n_row, b_rows, rank), f32),
             pltpu.VMEM((depth, rank), f32),
-            pltpu.VMEM((STEPS + 1, n_col, *tile), f32),
+            pltpu.VMEM((STEPS, n_col, *tile), f32),
             pltpu.VMEM((STEPS, n_col, *tile), f32),
             pltpu.VMEM((STEPS, n_row, *tile), f32),
             pltpu.VMEM((STEPS, n_col, *tile), f32),
+            pltpu.VMEM((n_col, *tile), f32),
             pltpu.VMEM((2, CHUNK * depth, rank), bf16),
             pltpu.VMEM((2, CHUNK * depth, rank), bf16),
             pltpu.VMEM((2, CHUNK * depth, second_here), bf16),
@@ -289,6 +314,8 @@
             collective_id=0, has_side_effects=True, vmem_limit_bytes=62 * 2**20
         ),
     )(observed, first_factor, second_factor, third_factor)
+    give = pl.pallas_call(hand_over, name="hand_over", out_shape=results, in_specs=[vmem] * 3, out_specs=[vmem] * 3)
+    return tuple(give(*factors))
 
 
 def solution(mesh):

time: 78.7 us -> 74.7 us (0.949)
  local copies, waits for them, and re-layouts: 4.07 us -> 0 us
    unnamed x3 -> x0, local copies, waits for them, and re-layouts: 4.07 us -> none
    pallas_call x0 -> x1, Pallas kernels: none -> 1.43 us  [per_device(): return tuple(give(*factors))]
    pallas_call x1, Pallas kernels: 73.6 us -> 72.4 us  [per_device(): pl.pallas_call(functools.partial(kernel, n_row, n_col, rates), name='cp_s...]
where the time goes in v1:
time: 74.7 us; the launch traced here: 74.5 us
  Pallas kernels  73.9 us (99%)
    pallas_call x1, Pallas kernels, per_device(): pl.pallas_call(functools.partial(kernel, n_row, n_col, rates), name='cp_s...  72.4 us

profile of v1, /device:TPU:1, one launch (start us, length us, event | category | flops | bytes accessed | tf_op | source)
XLA Modules:
  0.0 74.5 jit_solution(4159662903735341341)
XLA Ops:
  0.6 72.4 %cp_steps.1 = (f32[32,256]{1,0:T(8,128)}, f32[16,256]{1,0:T(8,128)}, f32[32,256]{1,0:T(8,128)}) custom-call(s32[256,32,256]{2,1,0:T(8,128)} %obs_hbm.1, f32[32,256]{1,0:T(8,128)} %a_in.1, f32[16,256]{1,0:T(8,128)} %b_in.1, f32[32,256]{1,0:T(8,128)} %c_in.1), custom_call_target="tpu_custom_call" | custom-call | tf_op jit(solution)/shard_map/cp_steps/pallas_call | solution.py:281
  73.1 1.4 %hand_over.1 = (f32[32,256]{1,0:T(8,128)}, f32[16,256]{1,0:T(8,128)}, f32[32,256]{1,0:T(8,128)}) custom-call(f32[32,256]{1,0:T(8,128)} %get-tuple-element.6.refs_0_, f32[16,256]{1,0:T(8,128)} %get-tuple-element.7.refs_1_, f32[32,256]{1,0:T(8,128)} %get-tuple-element.8.refs_2_), custom_call_target="tpu_custom_call" | custom-call | tf_op jit(solution)/shard_map/hand_over/pallas_call | solution.py:318

commit v2 on v1

--- a/solution.py
+++ b/solution.py
@@ -35,7 +35,7 @@
     obs, a_all, b_all, c_now, b_high, b_low, bt_high, bt_low,
     ga, ga_got, gb, gb_got, gc, gc_part, gc_got, gc_sum, c_new, c_tile,
     pair0, pair1, der0, der1,
-    obs_sem, a_send, a_recv, b_send, b_recv, ga_send, ga_recv, gb_send, gb_recv,
+    obs_sem, own_sem, a_send, a_recv, b_send, b_recv, ga_send, ga_recv, gb_send, gb_recv,
     c1_send, c1_recv, c2_send, c2_recv, c3_send, c3_recv,
 ):
     row, col = lax.axis_index("row"), lax.axis_index("col")
@@ -72,8 +72,17 @@
         pl.semaphore_signal(barrier, inc=1, device_id={"row": row_peer(d)}, device_id_type=MESH)
     for d in range(1, n_col):
         pl.semaphore_signal(barrier, inc=1, device_id={"col": col_peer(d)}, device_id_type=MESH)
+    own = [
+        pltpu.make_async_copy(b_in, b_all.at[0, row], own_sem.at[0]),
+        pltpu.make_async_copy(a_in, a_all.at[0, col], own_sem.at[1]),
+        pltpu.make_async_copy(c_in, c_now, own_sem.at[2]),
+    ]
+    for copy in own:
+        copy.start()
     for d in range(n_col):
         obs_copy(col_peer(d)).start()
+    for copy in own:
+        copy.wait()
     pl.semaphore_wait(barrier, n_row + n_col - 2)
 
     def send_b(step, src):
@@ -88,11 +97,16 @@
         here = a_all.at[step, block]
         to_col(here, here, a_send.at[step, 0], a_recv.at[step, block], col_peer(1)).wait_recv()
 
-    send_b(0, b_in)
-    send_a(0, a_in)
-    a_all[0, col] = a_in[...]
-    b_all[0, row] = b_in[...]
-    c_now[...] = c_in[...]
+    send_b(0, b_all.at[0, row])
+    send_a(0, a_all.at[0, col])
+
+    def c_arrived(step):
+        for d in range(1, n_col):
+            here = c_new.at[step, col_peer(d)]
+            to_col(here, here, c3_send.at[step, 0], c3_recv.at[step, col_peer(d)], col_peer(1)).wait_recv()
+        target = c_out if step + 1 == STEPS else c_now
+        for t, (k, l) in enumerate(tiles):
+            target[k * SUBLANES : (k + 1) * SUBLANES, l * LANES : (l + 1) * LANES] = c_new[step, t]
 
     def all_left(step):
         for d in range(1, n_col):
@@ -105,14 +119,14 @@
                 to_row(here, here, sem.at[step, d], gb_recv.at[step, 0], row_peer(d)).wait_send()
 
     for step in range(STEPS):
+        gb[step] = jnp.zeros(gb.shape[1:], f32)
+        gc[...] = jnp.zeros(gc.shape, f32)
         for d in range(1, n_row):
             here = b_all.at[step, row_peer(d)]
             to_row(here, here, b_send.at[step, 0], b_recv.at[step, row_peer(d)], row_peer(1)).wait_recv()
         halved = 0.5 * b_all[step].reshape(n_row * b_in.shape[0], rank)
         b_high[...], b_low[...] = split(halved)
         bt_high[...], bt_low[...] = split(halved.T)
-        gb[step] = jnp.zeros(gb.shape[1:], f32)
-        gc[...] = jnp.zeros(gc.shape, f32)
 
         def rows_of(block, half):
             return a_all[step, block, pl.ds(half * CHUNK, CHUNK), :]
@@ -146,6 +160,8 @@
 
         if step == 0:
             obs_copy(col).wait()
+        else:
+            c_arrived(step - 1)
         front(col, 0, pair0, der0)
 
         def block_body(d, carry):
@@ -250,12 +266,8 @@
             {"a": update_a, "b": update_b, "c": finish_c}[stage]()
         if final:
             all_left(step)
-        for d in range(1, n_col):
-            here = c_new.at[step, col_peer(d)]
-            to_col(here, here, c3_send.at[step, 0], c3_recv.at[step, col_peer(d)], col_peer(1)).wait_recv()
-        target = c_out if final else c_now
-        for t, (k, l) in enumerate(tiles):
-            target[k * SUBLANES : (k + 1) * SUBLANES, l * LANES : (l + 1) * LANES] = c_new[step, t]
+        if final:
+            c_arrived(step)
 
 
 def hand_over(*refs):
@@ -282,7 +294,7 @@
         functools.partial(kernel, n_row, n_col, rates),
         name="cp_steps",
         out_shape=results,
-        in_specs=[pl.BlockSpec(memory_space=pl.ANY), vmem, vmem, vmem],
+        in_specs=[pl.BlockSpec(memory_space=pl.ANY)] * 4,
         out_specs=[vmem] * 3,
         scratch_shapes=[
             pltpu.VMEM(observed.shape, jnp.int32),
@@ -308,6 +320,7 @@
             pltpu.VMEM((2, CHUNK * depth, second_here), bf16),
             pltpu.VMEM((2, CHUNK * depth, second_here), bf16),
             dma((n_col,)),
+            dma((3,)),
         ]
         + [dma((STEPS, n)) for n in (n_col, n_row, n_col, n_row, n_col, n_row, n_col) for _ in range(2)],
         compiler_params=pltpu.CompilerParams(

time: 74.7 us -> 74.2 us (level)
  no operation moved by 1% of the time
where the time goes in v2:
time: 74.2 us; the launch traced here: 74 us
  Pallas kernels  73.4 us (99%)
    pallas_call x1, Pallas kernels, per_device(): pl.pallas_call(functools.partial(kernel, n_row, n_col, rates), name='cp_s...  72 us

profile of v2, /device:TPU:1, one launch (start us, length us, event | category | flops | bytes accessed | tf_op | source)
XLA Modules:
  0.0 74.0 jit_solution(6974541609370526226)
XLA Ops:
  0.6 72.0 %cp_steps.1 = (f32[32,256]{1,0:T(8,128)}, f32[16,256]{1,0:T(8,128)}, f32[32,256]{1,0:T(8,128)}) custom-call(s32[256,32,256]{2,1,0:T(8,128)} %obs_hbm.1, f32[32,256]{1,0:T(8,128)} %a_in.1, f32[16,256]{1,0:T(8,128)} %b_in.1, f32[32,256]{1,0:T(8,128)} %c_in.1), custom_call_target="tpu_custom_call" | custom-call | tf_op jit(solution)/shard_map/cp_steps/pallas_call | solution.py:293
  72.6 1.4 %hand_over.1 = (f32[32,256]{1,0:T(8,128)}, f32[16,256]{1,0:T(8,128)}, f32[32,256]{1,0:T(8,128)}) custom-call(f32[32,256]{1,0:T(8,128)} %get-tuple-element.6.refs_0_, f32[16,256]{1,0:T(8,128)} %get-tuple-element.7.refs_1_, f32[32,256]{1,0:T(8,128)} %get-tuple-element.8.refs_2_), custom_call_target="tpu_custom_call" | custom-call | tf_op jit(solution)/shard_map/hand_over/pallas_call | solution.py:331
